TPU v7x, 256 devices: a whole 4x4x8 slice. The times are simulated.
256 devices in a mesh: expert: 32 (over x, y, z_hi), tok: 8 (over z_lo, core).
Axes of the slice: x: 4, y: 4, z: 8 (z_hi: 2, z_lo: 4; z = z_hi * 4 + z_lo), core: 2. Of those that a mesh axis runs over, the one named last changes fastest.
Arguments:
- tokens: bfloat16 [8192, 7168], P(('tok', 'expert')), may hold values from -6 to 6
- w_gate: bfloat16 [64, 7168, 1024], P('expert', None, 'tok'), may hold values from -0.0625 to 0.0625
- w_up: bfloat16 [64, 7168, 1024], P('expert', None, 'tok'), may hold values from -0.0625 to 0.0625
- w_down: bfloat16 [64, 1024, 7168], P('expert', 'tok'), may hold values from -0.1875 to 0.1875
- gates: float32 [8, 64, 32], replicated, may hold values from 0.2 to 1
- dispatch: int32 [8, 64, 32], replicated, may hold values from 0 to 1023, as said below
Outputs:
- combined: bfloat16 [8192, 7168], P(('tok', 'expert'))
Inputs may be any that keep to these rules, and one draw needn't show every extreme that they name: `dispatch`: for each step and expert the 32 indices are different, and at most 2 of them lie in one aligned block of 32 indices (the rows of one device); in every step and for every expert some block holds exactly 2.
All inputs are finite; a program needn't handle non-finite values.
Results may differ from a plain program's by a relative error of at most 0.015.
Values may be sent and summed in bfloat16 or wider, within the bound.
A program may use at most 128 MiB of HBM per device.

v0:
```python
import jax
import jax.numpy as jnp
from jax import lax
from jax.sharding import Mesh
from jax.sharding import PartitionSpec as P

MOST = 2
TOK = ("tok_0", "tok_1")
TOK_EXPERT = ("tok_0", "tok_1", "expert")


def sum_in_order(tiles, axes, turns):
    dims = [lax.axis_size(a) for a in axes]
    tiles = tiles.reshape(*dims, *tiles.shape[1:])
    tiles = tiles.transpose(*turns, *range(len(axes), tiles.ndim))
    tiles = tiles.reshape(-1, *tiles.shape[len(axes) :])
    for k in turns:
        tiles = lax.psum_scatter(tiles, axes[k], scatter_dimension=0, tiled=True)
    return tiles[0]


def cut_along(array, dim, devices):
    before, after = (array.shape[:dim], array.shape[dim + 1 :])
    return jnp.moveaxis(array.reshape(*before, devices, -1, *after), dim, 0)


def scatter_axes(array, axes, turns, dim):
    devices = lax.axis_size(axes)
    return sum_in_order(cut_along(array, dim, devices), axes, turns)


def route_tables(dispatch, rows_dev):
    source = dispatch // rows_dev
    offset = dispatch % rows_dev
    position = jnp.arange(dispatch.shape[-1])
    earlier = (source[..., :, None] == source[..., None, :]) & (
        position[None, :] < position[:, None]
    )
    within = jnp.sum(earlier.astype(jnp.int32), axis=-1)
    return (source, offset, within)


def owner_select(source, offset, within, owner_idx, rows_dev, per_source):
    taken = (
        (source == owner_idx)[..., None] & (within[..., None] == jnp.arange(per_source))
    ).astype(jnp.bfloat16)
    row_table = (offset[..., None] == jnp.arange(rows_dev)).astype(jnp.bfloat16)
    picker = jnp.einsum("ecm,ecr->emr", taken, row_table, preferred_element_type=jnp.float32)
    return picker.astype(jnp.bfloat16).reshape(-1, rows_dev)


def slot_table(source, within, sources, per_source):
    match_source = source[..., None, None] == jnp.arange(sources)[:, None]
    match_within = within[..., None, None] == jnp.arange(per_source)[None, :]
    return (match_source & match_within).astype(jnp.bfloat16)


def expert_partial(chosen, w_gate, w_up, w_down, weight):
    gate_pre = jnp.einsum("...ecd,edh->...ech", chosen, w_gate, preferred_element_type=jnp.float32)
    up_pre = jnp.einsum("...ecd,edh->...ech", chosen, w_up, preferred_element_type=jnp.float32)
    hidden = (jax.nn.silu(gate_pre) * up_pre).astype(jnp.bfloat16)
    down_out = jnp.einsum("...ech,ehd->...ecd", hidden, w_down, preferred_element_type=jnp.float32)
    return (down_out * weight[..., None]).astype(jnp.bfloat16)


def body(tokens, w_gate, w_up, w_down, gates, dispatch):
    sources = lax.axis_size("expert")
    owners = lax.axis_size(TOK)
    rows_dev = tokens.shape[0]
    model_width = tokens.shape[1]
    exp_dev = w_gate.shape[0]
    per_source = MOST
    self_idx = lax.axis_index("expert")
    source, offset, within = route_tables(dispatch, rows_dev)
    mine_source = lax.dynamic_slice_in_dim(source, self_idx * exp_dev, exp_dev, 1)
    mine_within = lax.dynamic_slice_in_dim(within, self_idx * exp_dev, exp_dev, 1)
    gate_mine = lax.dynamic_slice_in_dim(gates, self_idx * exp_dev, exp_dev, 1)
    slots_mine = slot_table(mine_source, mine_within, sources, per_source)
    owner_idx = lax.axis_index(TOK)
    own_source = lax.dynamic_index_in_dim(source, owner_idx, 0, keepdims=False)
    own_offset = lax.dynamic_index_in_dim(offset, owner_idx, 0, keepdims=False)
    own_within = lax.dynamic_index_in_dim(within, owner_idx, 0, keepdims=False)
    picker = owner_select(own_source, own_offset, own_within, self_idx, rows_dev, per_source)
    outgoing = jnp.dot(picker, tokens, preferred_element_type=jnp.float32).astype(jnp.bfloat16)
    outgoing = outgoing.reshape(sources, exp_dev * per_source, model_width)
    arrived = lax.all_to_all(outgoing, "expert", split_axis=0, concat_axis=0, tiled=True)
    everyone = lax.all_gather(arrived[None], TOK, axis=0, tiled=True)
    everyone = everyone.reshape(owners, sources, exp_dev, per_source, model_width)
    chosen = jnp.einsum(
        "secpk,spekd->secd", slots_mine, everyone, preferred_element_type=jnp.float32
    ).astype(jnp.bfloat16)
    partial_value = expert_partial(chosen, w_gate, w_up, w_down, gate_mine)
    summed = scatter_axes(partial_value, TOK, (1, 0), 0).astype(jnp.float32)[0].astype(jnp.bfloat16)
    own_slots = lax.dynamic_index_in_dim(slots_mine, owner_idx, 0, keepdims=False)
    returning = jnp.einsum(
        "ecpk,ecd->pekd", own_slots, summed, preferred_element_type=jnp.float32
    ).astype(jnp.bfloat16)
    returning = returning.reshape(sources, exp_dev * per_source, model_width)
    returned = lax.all_to_all(returning, "expert", split_axis=0, concat_axis=0, tiled=True)
    returned = returned.reshape(sources * exp_dev * per_source, model_width)
    return jnp.dot(picker.T, returned, preferred_element_type=jnp.float32).astype(jnp.bfloat16)


def solution(mesh):
    split = Mesh(mesh.devices.reshape(mesh.shape["expert"], 4, 2), ("expert", "tok_0", "tok_1"))
    in_specs = (
        P(TOK_EXPERT, None),
        P("expert", None, TOK),
        P("expert", None, TOK),
        P("expert", TOK, None),
        P(),
        P(),
    )
    out_specs = P(TOK_EXPERT, None)
    return jax.shard_map(body, mesh=split, in_specs=in_specs, out_specs=out_specs, check_vma=False)
```

profile of v0, /device:TPU:64, one launch (start us, length us, event | category | flops | bytes accessed | tf_op | source)
XLA Modules:
  0.0 428.7 jit_solution(624430313209946607)
XLA Ops:
  6.5 1.0 add_select_fusion
  7.6 1.0 broadcast_compare_fusion
  8.6 1.2 convert_reduce_fusion
  10.0 0.5 convolution_convert_fusion.3
  10.5 1.9 convolution_convert_fusion.1
  12.3 3.1 reshape.65
  15.5 61.8 %all_to_all.10 = bf16[32,4,7168]{2,1,0:T(4,128)(2,1)S(1)} all-to-all(bf16[32,4,7168]{2,1,0:T(4,128)(2,1)S(1)} %reshape.65), channel_id=1, replica_groups=mesh['expert'=32,'tok_0'=4,'tok_1'=2] {'expert'}, dimensions={0} | all-to-all | bytes 3670016 | tf_op jit(solution)/shard_map/all_to_all | solution.py:86
  77.2 1.8 copy.57
  79.0 0.2 reduce-scatter.3.cloned.1.call-start
  79.9 0.1 iota_compare_fusion.2
  80.0 143.8 %all-gather.3.cloned.1.call-done = bf16[256,4,7168]{2,0,1:T(8,128)(2,1)} async-done(((bf16[32,4,7168]{2,0,1:T(8,128)(2,1)}), bf16[256,4,7168]{2,0,1:T(8,128)(2,1)}) %all-gather.3.cloned.1.call-update) | async-done | bytes 14680080 | tf_op jit(solution)/shard_map/all_gather | solution.py:87
  223.8 6.6 %bitcast_convert_fusion = bf16[8,2,32,7168]{3,2,1,0:T(8,128)(2,1)S(1)} fusion(bf16[8,32,2,2,7168]{4,1,0,3,2:T(8,128)(2,1)} %bitcast.74, pred[8,2,32,2]{2,3,1,0:T(4,128)(4,1)S(1)} %iota_compare_fusion.3, pred[8,2,32,32]{3,2,1,0:T(8,128)(4,1)S(1)} %iota_compare_fusion.2), kind=kOutput, calls=%fused_computation.2 | convolution fusion | flops 473464832 | bytes 22037504 | tf_op jit(solution)/shard_map/secpk,spekd->secd/dot_general | solution.py:89
  230.4 3.0 copy-done.2
  233.4 2.1 fusion.12
  235.5 12.2 %fusion = bf16[8,2,32,7168]{3,2,0,1:T(8,128)(2,1)} fusion(f32[8,2,32]{2,0,1:T(8,128)S(1)} %copy.61, bf16[2,128,7168]{2,1,0:T(8,128)(2,1)} %param.9, bf16[2,7168,128]{2,1,0:T(8,128)(2,1)} %param.8, bf16[8,2,32,7168]{3,2,1,0:T(8,128)(2,1)} %copy-done.2, f32[8,2,32,128]{3,2,0,1:T(8,128)S(1)} %fusion.12), kind=kOutput, calls=%fused_computation.1 | convolution fusion | flops 1886781440 | bytes 22284288 | tf_op jit(solution)/shard_map/...ech,ehd->...ecd/dot_general | solution.py:62
  247.7 6.7 %copy.62 = bf16[2,4,1,2,32,7168]{5,4,3,1,0,2:T(8,128)(2,1)} copy(bf16[2,4,1,2,32,7168]{5,4,0,1,3,2:T(8,128)(2,1)} %bitcast.73) | data formatting | bytes 14680064 | tf_op jit(solution)/shard_map/transpose | solution.py:15
  254.5 23.0 %reduce-scatter.3.cloned.1.call-done = bf16[4,1,2,32,7168]{4,3,2,1,0:T(8,128)(2,1)} async-done(((bf16[8,1,2,32,7168]{4,3,2,1,0:T(8,128)(2,1)}), bf16[4,1,2,32,7168]{4,3,2,1,0:T(8,128)(2,1)}) %reduce-scatter.3.cloned.1.call-update) | async-done | bytes 3670032 | tf_op jit(solution)/shard_map/reduce_scatter | solution.py:18
  277.5 0.2 broadcast_and_fusion
  277.7 77.6 %reduce-scatter.5.cloned.1.call-done = bf16[1,1,2,32,7168]{4,3,2,1,0:T(8,128)(2,1)} async-done(((bf16[4,1,2,32,7168]{4,3,2,1,0:T(8,128)(2,1)}), bf16[1,1,2,32,7168]{4,3,2,1,0:T(8,128)(2,1)}) %reduce-scatter.5.cloned.1.call-update) | async-done | bytes 917520 | tf_op jit(solution)/shard_map/reduce_scatter | solution.py:18
  355.3 1.8 convolution_convert_fusion
  357.2 1.4 copy.64
  358.6 59.4 %all_to_all.11 = bf16[32,4,7168]{2,1,0:T(4,128)(2,1)} all-to-all(bf16[32,4,7168]{2,1,0:T(4,128)(2,1)S(1)} %copy.64), channel_id=1, replica_groups=mesh['expert'=32,'tok_0'=4,'tok_1'=2] {'expert'}, dimensions={0} | all-to-all | bytes 3670016 | tf_op jit(solution)/shard_map/all_to_all | solution.py:99
  418.0 2.9 reshape.69
  421.0 1.2 convolution_convert_fusion.2
  (26 shorter events, 1.0 us)
Async XLA Ops:
  6.5 3.9 copy-start
  6.5 217.3 %all-gather.3.cloned.1.call-start = ((), (), s32[]{:S(2)}) async-start(), calls=%async_computation.6 | async-start | bytes 16515072 | tf_op jit(solution)/shard_map/all_gather | solution.py:87
  77.2 2.4 copy-start.3
  79.0 198.5 %reduce-scatter.3.cloned.1.call-start = ((), (), s32[]{:S(2)}) async-start(), calls=%async_computation.4 | async-start | bytes 11010048 | tf_op jit(solution)/shard_map/reduce_scatter | solution.py:18
  223.8 9.6 %copy-start.4 = (bf16[2,7168,128]{2,1,0:T(8,128)(2,1)S(1)}, bf16[2,7168,128]{2,1,0:T(8,128)(2,1)}, u32[]{:S(2)}) copy-start(bf16[2,7168,128]{2,1,0:T(8,128)(2,1)} %param.7) | copy-start | bytes 11010052
  230.4 3.0 copy-start.2
  254.4 100.9 %reduce-scatter.5.cloned.1.call-start = ((), (), s32[]{:S(2)}) async-start(), calls=%async_computation.5 | async-start | bytes 4587520 | tf_op jit(solution)/shard_map/reduce_scatter | solution.py:18
  358.6 63.5 %copy-start.1 = (bf16[32,7168]{1,0:T(8,128)(2,1)S(1)}, bf16[32,7168]{1,0:T(8,128)(2,1)}, u32[]{:S(2)}) copy-start(bf16[32,7168]{1,0:T(8,128)(2,1)} %param.6) | copy-start | bytes 1376260
Sparse Core Ops, SparseCore 0:
  79.2 144.5 all-gather.2
  254.6 22.8 reduce-scatter.2
  280.1 75.2 reduce-scatter.4
where the time goes:
time: 429 us
  waiting for transfers between devices  244 us (57%)
  blocking collectives  121 us (28%)
  matrix products  26.2 us (6%)
  local copies, waits for them, and re-layouts  19.8 us (5%)
  between operations  13.3 us (3%)
    all_gather x1, waiting for transfers between devices, body(): everyone = lax.all_gather(arrived[None], TOK, axis=0, tiled=True)  144 us
    reduce_scatter x2, waiting for transfers between devices, sum_in_order(): tiles = lax.psum_scatter(tiles, axes[k], scatter_dimension=0, tiled=True)  101 us
    all_to_all x1, blocking collectives, body(): lax.all_to_all(outgoing, 'expert', split_axis=0, concat_axis=0, tiled=True)  61.8 us
    all_to_all x1, blocking collectives, body(): lax.all_to_all(returning, 'expert', split_axis=0, concat_axis=0, tiled=True)  59.4 us
    dot_general x1, matrix products, expert_partial(): jnp.einsum('...ech,ehd->...ecd', hidden, w_down, preferred_element_type=j...  12.2 us
  transfers between devices with their start and end apart: 3, of which 3 were waited for; matrix products, arithmetic and copies ran while one was open for 0% of the time, Pallas kernels for 0%

commit v1 on v0

--- a/solution.py
+++ b/solution.py
@@ -3,6 +3,7 @@
 from jax import lax
 from jax.sharding import Mesh
 from jax.sharding import PartitionSpec as P
+from jax.lax import all_to_all, psum
 
 MOST = 2
 TOK = ("tok_0", "tok_1")
@@ -84,7 +85,10 @@
     outgoing = jnp.dot(picker, tokens, preferred_element_type=jnp.float32).astype(jnp.bfloat16)
     outgoing = outgoing.reshape(sources, exp_dev * per_source, model_width)
     arrived = lax.all_to_all(outgoing, "expert", split_axis=0, concat_axis=0, tiled=True)
-    everyone = lax.all_gather(arrived[None], TOK, axis=0, tiled=True)
+    inner_x = arrived[None]
+    everyone = jnp.concatenate(
+        all_to_all(jnp.stack([inner_x for _ in range(psum(1, TOK))], axis=0), TOK, 0, 0), axis=0
+    )
     everyone = everyone.reshape(owners, sources, exp_dev, per_source, model_width)
     chosen = jnp.einsum(
         "secpk,spekd->secd", slots_mine, everyone, preferred_element_type=jnp.float32

time: 429 us -> 606 us (1.41)
  waiting for transfers between devices: 244 us -> 409 us
  starting transfers between devices: 0.27 us -> 6.37 us
    all_to_all x0 -> x1, waiting for transfers between devices: none -> 315 us  [body(): all_to_all(jnp.stack([inner_x for _ in range(psum(1, TOK))], axis=0), TOK...]
    all_gather x1 -> x0, waiting for transfers between devices: 144 us -> none  [body(): everyone = lax.all_gather(arrived[None], TOK, axis=0, tiled=True)]
    all_to_all x0 -> x1, starting transfers between devices: none -> 6.32 us  [body(): all_to_all(jnp.stack([inner_x for _ in range(psum(1, TOK))], axis=0), TOK...]
where the time goes in v1:
time: 606 us; the launch traced here: 605 us
  waiting for transfers between devices  409 us (67%)
  blocking collectives  121 us (20%)
  matrix products  27.1 us (4%)
  local copies, waits for them, and re-layouts  24.1 us (4%)
  between operations  13.6 us (2%)
  starting transfers between devices  6.37 us (1%)
    all_to_all x1, waiting for transfers between devices, body(): all_to_all(jnp.stack([inner_x for _ in range(psum(1, TOK))], axis=0), TOK...  315 us
    reduce_scatter x2, waiting for transfers between devices, sum_in_order(): tiles = lax.psum_scatter(tiles, axes[k], scatter_dimension=0, tiled=True)  94.8 us
    all_to_all x1, blocking collectives, body(): lax.all_to_all(outgoing, 'expert', split_axis=0, concat_axis=0, tiled=True)  61.8 us
    all_to_all x1, blocking collectives, body(): lax.all_to_all(returning, 'expert', split_axis=0, concat_axis=0, tiled=True)  59.4 us
    dot_general x1, matrix products, expert_partial(): jnp.einsum('...ech,ehd->...ecd', hidden, w_down, preferred_element_type=j...  12.2 us
  transfers between devices with their start and end apart: 3, of which 3 were waited for; matrix products, arithmetic and copies ran while one was open for 0% of the time, Pallas kernels for 0%

profile of v1, /device:TPU:64, one launch (start us, length us, event | category | flops | bytes accessed | tf_op | source)
XLA Modules:
  0.0 605.3 jit_solution(17813312646963426684)
XLA Ops:
  6.5 1.0 broadcast_compare_fusion
  7.6 1.0 add_select_fusion
  8.7 1.2 convert_reduce_fusion
  10.0 0.5 convolution_convert_fusion.3
  10.5 1.9 convolution_convert_fusion.1
  12.3 3.1 reshape.64
  15.5 61.8 %all_to_all.15 = bf16[32,4,7168]{2,1,0:T(4,128)(2,1)S(1)} all-to-all(bf16[32,4,7168]{2,1,0:T(4,128)(2,1)S(1)} %reshape.64), channel_id=1, replica_groups=mesh['expert'=32,'tok_0'=4,'tok_1'=2] {'expert'}, dimensions={0} | all-to-all | bytes 3670016 | tf_op jit(solution)/shard_map/all_to_all | solution.py:87
  77.2 0.5 copy.55
  77.8 5.5 stack.3
  83.3 6.3 %all-to-all-start.1 = ((bf16[8,1,32,4,7168]{4,2,3,1,0:T(8,128)(2,1)}), bf16[8,1,32,4,7168]{4,2,3,1,0:T(8,128)(2,1)}, u32[]{:S(2)}, u32[]{:S(2)}) async-start(bf16[8,1,32,4,7168]{4,2,3,1,0:T(8,128)(2,1)} %stack.3), calls=%async_computation.1 | async-start | bytes 29360128 | tf_op jit(solution)/shard_map/all_to_all | solution.py:90
  90.4 314.6 %all-to-all-done.1 = bf16[8,1,32,4,7168]{4,2,3,1,0:T(8,128)(2,1)} async-done(((bf16[8,1,32,4,7168]{4,2,3,1,0:T(8,128)(2,1)}), bf16[8,1,32,4,7168]{4,2,3,1,0:T(8,128)(2,1)}, u32[]{:S(2)}, u32[]{:S(2)}) %all-to-all-start.1) | async-done | bytes 14680096 | tf_op jit(solution)/shard_map/all_to_all | solution.py:90
  405.0 7.5 %bitcast_convert_fusion = bf16[8,2,32,7168]{3,2,1,0:T(8,128)(2,1)S(1)} fusion(bf16[8,32,2,2,7168]{4,1,3,2,0:T(8,128)(2,1)} %bitcast.4, pred[8,2,32,2]{2,3,1,0:T(4,128)(4,1)S(1)} %iota_compare_fusion.3, pred[8,2,32,32]{3,2,1,0:T(8,128)(4,1)S(1)} %iota_compare_fusion.2), kind=kOutput, calls=%fused_computation.2 | convolution fusion | flops 473464832 | bytes 22037504 | tf_op jit(solution)/shard_map/secpk,spekd->secd/dot_general | solution.py:93
  412.6 3.0 copy-done.2
  415.6 2.1 fusion.8
  417.6 12.2 %fusion = bf16[8,2,32,7168]{3,2,0,1:T(8,128)(2,1)} fusion(f32[8,2,32]{2,0,1:T(8,128)S(1)} %copy.58, bf16[2,128,7168]{2,1,0:T(8,128)(2,1)} %param.9, bf16[2,7168,128]{2,1,0:T(8,128)(2,1)} %param.8, bf16[8,2,32,7168]{3,2,1,0:T(8,128)(2,1)} %copy-done.2, f32[8,2,32,128]{3,2,0,1:T(8,128)S(1)} %fusion.8), kind=kOutput, calls=%fused_computation.1 | convolution fusion | flops 1886781440 | bytes 22284288 | tf_op jit(solution)/shard_map/...ech,ehd->...ecd/dot_general | solution.py:63
  429.8 6.7 %copy.59 = bf16[2,4,1,2,32,7168]{5,4,3,1,0,2:T(8,128)(2,1)} copy(bf16[2,4,1,2,32,7168]{5,4,0,1,3,2:T(8,128)(2,1)} %bitcast.74) | data formatting | bytes 14680064 | tf_op jit(solution)/shard_map/transpose | solution.py:16
  436.6 17.2 %reduce-scatter.3.cloned.1.call-done = bf16[4,1,2,32,7168]{4,3,2,1,0:T(8,128)(2,1)} async-done(((bf16[8,1,2,32,7168]{4,3,2,1,0:T(8,128)(2,1)}), bf16[4,1,2,32,7168]{4,3,2,1,0:T(8,128)(2,1)}) %reduce-scatter.3.cloned.1.call-update) | async-done | bytes 3670032 | tf_op jit(solution)/shard_map/reduce_scatter | solution.py:19
  453.9 0.2 broadcast_and_fusion
  454.1 77.6 %reduce-scatter.5.cloned.1.call-done = bf16[1,1,2,32,7168]{4,3,2,1,0:T(8,128)(2,1)} async-done(((bf16[4,1,2,32,7168]{4,3,2,1,0:T(8,128)(2,1)}), bf16[1,1,2,32,7168]{4,3,2,1,0:T(8,128)(2,1)}) %reduce-scatter.5.cloned.1.call-update) | async-done | bytes 917520 | tf_op jit(solution)/shard_map/reduce_scatter | solution.py:19
  531.7 1.9 convolution_convert_fusion
  533.5 1.4 copy.61
  535.0 59.4 %all_to_all.16 = bf16[32,4,7168]{2,1,0:T(4,128)(2,1)} all-to-all(bf16[32,4,7168]{2,1,0:T(4,128)(2,1)S(1)} %copy.61), channel_id=1, replica_groups=mesh['expert'=32,'tok_0'=4,'tok_1'=2] {'expert'}, dimensions={0} | all-to-all | bytes 3670016 | tf_op jit(solution)/shard_map/all_to_all | solution.py:103
  594.3 2.9 reshape.67
  597.3 1.2 convolution_convert_fusion.2
  (26 shorter events, 1.1 us)
Async XLA Ops:
  6.5 3.9 copy-start
  83.3 6.3 %copy-start.3 = (f32[8,64,32]{1,2,0:T(8,128)S(1)}, f32[8,64,32]{1,2,0:T(8,128)}, u32[]{:S(2)}) copy-start(f32[8,64,32]{1,2,0:T(8,128)} %param.10) | copy-start | bytes 196612
  83.3 321.7 %all-to-all-start.1 = ((bf16[8,1,32,4,7168]{4,2,3,1,0:T(8,128)(2,1)}), bf16[8,1,32,4,7168]{4,2,3,1,0:T(8,128)(2,1)}, u32[]{:S(2)}, u32[]{:S(2)}) async-start(bf16[8,1,32,4,7168]{4,2,3,1,0:T(8,128)(2,1)} %stack.3), calls=%async_computation.1 | async-start | bytes 29360128 | tf_op jit(solution)/shard_map/all_to_all | solution.py:90
  89.6 364.2 %reduce-scatter.3.cloned.1.call-start = ((), (), s32[]{:S(2)}) async-start(), calls=%async_computation.5 | async-start | bytes 11010048 | tf_op jit(solution)/shard_map/reduce_scatter | solution.py:19
  405.0 10.6 %copy-start.4 = (bf16[2,7168,128]{2,1,0:T(8,128)(2,1)S(1)}, bf16[2,7168,128]{2,1,0:T(8,128)(2,1)}, u32[]{:S(2)}) copy-start(bf16[2,7168,128]{2,1,0:T(8,128)(2,1)} %param.7) | copy-start | bytes 11010052
  412.6 3.0 copy-start.2
  436.6 95.1 %reduce-scatter.5.cloned.1.call-start = ((), (), s32[]{:S(2)}) async-start(), calls=%async_computation.6 | async-start | bytes 4587520 | tf_op jit(solution)/shard_map/reduce_scatter | solution.py:19
  534.9 63.5 %copy-start.1 = (bf16[32,7168]{1,0:T(8,128)(2,1)S(1)}, bf16[32,7168]{1,0:T(8,128)(2,1)}, u32[]{:S(2)}) copy-start(bf16[32,7168]{1,0:T(8,128)(2,1)} %param.6) | copy-start | bytes 1376260
Sparse Core Ops, SparseCore 0:
  436.7 17.1 reduce-scatter.2
  456.4 75.2 reduce-scatter.4
